TPU v7x, 32 devices: a whole 2x2x4 slice. The times are simulated.
32 devices in a mesh: gx: 4 (over z), gy: 8 (over y, x, core).
Axes of the slice: x: 2, y: 2, z: 4, core: 2. Of those that a mesh axis runs over, the one named last changes fastest.
Arguments:
- tokens: bfloat16 [33856, 768], P(('gx', 'gy')), may hold values from -6 to 6
- lengths: int32 [64], P(('gx', 'gy')), may hold values from 40 to 529, as said below
- key_mask: int32 [64, 529], P(('gx', 'gy')), may hold values 0 or 1
- ln1_gain: bfloat16 [768], P(('gx', 'gy')), may hold values from 0.5 to 1.5
- ln1_bias: bfloat16 [768], P(('gx', 'gy')), may hold values from -1.1953125 to 1.1953125
- q_weight: bfloat16 [768, 768], P(('gx', 'gy')), may hold values from -0.21875 to 0.21875
- q_bias: bfloat16 [768], P(('gx', 'gy')), may hold values from -1.1953125 to 1.1953125
- k_weight: bfloat16 [768, 768], P(('gx', 'gy')), may hold values from -0.21875 to 0.21875
- v_weight: bfloat16 [768, 768], P(('gx', 'gy')), may hold values from -0.21875 to 0.21875
- v_bias: bfloat16 [768], P(('gx', 'gy')), may hold values from -1.1953125 to 1.1953125
- o_weight: bfloat16 [768, 768], P(('gx', 'gy')), may hold values from -3.5 to 3.5
- o_bias: bfloat16 [768], P(('gx', 'gy')), may hold values from -1.1953125 to 1.1953125
- ln2_gain: bfloat16 [768], P(('gx', 'gy')), may hold values from 0.5 to 1.5
- ln2_bias: bfloat16 [768], P(('gx', 'gy')), may hold values from -1.1953125 to 1.1953125
- up_weight: bfloat16 [768, 3072], P(('gx', 'gy')), may hold values from -0.21875 to 0.21875
- up_bias: bfloat16 [3072], P(('gx', 'gy')), may hold values from -1.1953125 to 1.1953125
- down_weight: bfloat16 [3072, 768], P(('gx', 'gy')), may hold values from -0.21875 to 0.21875
- down_bias: bfloat16 [768], P(('gx', 'gy')), may hold values from -1.1953125 to 1.1953125
- out_grad: bfloat16 [33856, 768], P(('gx', 'gy')), may hold values from -6 to 6
Outputs:
- block_out: bfloat16 [33856, 768], P(('gx', 'gy'))
- grad_tokens: float32 [33856, 768], P(('gx', 'gy'))
- grad_ln1_gain: float32 [768], P(('gx', 'gy'))
- grad_ln1_bias: float32 [768], P(('gx', 'gy'))
- grad_q_weight: float32 [768, 768], P(('gx', 'gy'))
- grad_q_bias: float32 [768], P(('gx', 'gy'))
- grad_k_weight: float32 [768, 768], P(('gx', 'gy'))
- grad_v_weight: float32 [768, 768], P(('gx', 'gy'))
- grad_v_bias: float32 [768], P(('gx', 'gy'))
- grad_o_weight: float32 [768, 768], P(('gx', 'gy'))
- grad_o_bias: float32 [768], P(('gx', 'gy'))
- grad_ln2_gain: float32 [768], P(('gx', 'gy'))
- grad_ln2_bias: float32 [768], P(('gx', 'gy'))
- grad_up_weight: float32 [768, 3072], P(('gx', 'gy'))
- grad_up_bias: float32 [3072], P(('gx', 'gy'))
- grad_down_weight: float32 [3072, 768], P(('gx', 'gy'))
- grad_down_bias: float32 [768], P(('gx', 'gy'))
Inputs may be any that keep to these rules, and one draw needn't show every extreme that they name: `lengths`: most strips are nearly full, and strip 0 holds 529 filled slots.
All inputs are finite; a program needn't handle non-finite values. No bound on the sum of `key_mask` on one device may be relied on, other than what follows from the above.
Results may differ from a plain program's by a relative error of at most 0.012.
Values may be sent and summed in bfloat16 or wider, within the bound.
A program may use at most 192 MiB of HBM per device.

v0:
```python
import math
import jax
import jax.numpy as jnp
from jax import lax
from jax.sharding import PartitionSpec as P

HEAD_DIM = 64
EPSILON = 1e-06
NEG_FILL = -1e30


def layer_norm(values, gain_vec, bias_vec):
    center = values - jnp.mean(values, axis=-1, keepdims=True)
    spread = jnp.mean(center * center, axis=-1, keepdims=True)
    return center * lax.rsqrt(spread + EPSILON) * gain_vec + bias_vec


def gelu_exact(values):
    return jax.nn.gelu(values, approximate=False)


def right_mul(left_arg, right_arg):
    return jnp.dot(left_arg, right_arg, preferred_element_type=jnp.float32)


def left_mul(left_arg, right_arg):
    return lax.dot_general(
        left_arg, right_arg, (((0,), (0,)), ((), ())), preferred_element_type=jnp.float32
    )


def back_mul(left_arg, right_arg):
    return lax.dot_general(
        left_arg, right_arg, (((1,), (1,)), ((), ())), preferred_element_type=jnp.float32
    )


def collect(
    ln1_gain,
    ln1_bias,
    q_weight,
    q_bias,
    k_weight,
    v_weight,
    v_bias,
    o_weight,
    o_bias,
    ln2_gain,
    ln2_bias,
    up_weight,
    up_bias,
    down_weight,
    down_bias,
):
    return (
        lax.all_gather(ln1_gain, ("gx", "gy"), axis=0, tiled=True),
        lax.all_gather(ln1_bias, ("gx", "gy"), axis=0, tiled=True),
        lax.all_gather(q_weight, ("gx", "gy"), axis=0, tiled=True),
        lax.all_gather(q_bias, ("gx", "gy"), axis=0, tiled=True),
        lax.all_gather(k_weight, ("gx", "gy"), axis=0, tiled=True),
        lax.all_gather(v_weight, ("gx", "gy"), axis=0, tiled=True),
        lax.all_gather(v_bias, ("gx", "gy"), axis=0, tiled=True),
        lax.all_gather(o_weight, ("gx", "gy"), axis=0, tiled=True),
        lax.all_gather(o_bias, ("gx", "gy"), axis=0, tiled=True),
        lax.all_gather(ln2_gain, ("gx", "gy"), axis=0, tiled=True),
        lax.all_gather(ln2_bias, ("gx", "gy"), axis=0, tiled=True),
        lax.all_gather(up_weight, ("gx", "gy"), axis=0, tiled=True),
        lax.all_gather(up_bias, ("gx", "gy"), axis=0, tiled=True),
        lax.all_gather(down_weight, ("gx", "gy"), axis=0, tiled=True),
        lax.all_gather(down_bias, ("gx", "gy"), axis=0, tiled=True),
    )


def spread_grads(
    grad_g1,
    grad_b1,
    grad_wq,
    grad_bq,
    grad_wk,
    grad_wv,
    grad_bv,
    grad_wo,
    grad_bo,
    grad_g2,
    grad_b2,
    grad_wup,
    grad_bup,
    grad_wdown,
    grad_bdown,
):
    return (
        lax.psum_scatter(grad_g1, ("gx", "gy"), scatter_dimension=0, tiled=True),
        lax.psum_scatter(grad_b1, ("gx", "gy"), scatter_dimension=0, tiled=True),
        lax.psum_scatter(grad_wq, ("gx", "gy"), scatter_dimension=0, tiled=True),
        lax.psum_scatter(grad_bq, ("gx", "gy"), scatter_dimension=0, tiled=True),
        lax.psum_scatter(grad_wk, ("gx", "gy"), scatter_dimension=0, tiled=True),
        lax.psum_scatter(grad_wv, ("gx", "gy"), scatter_dimension=0, tiled=True),
        lax.psum_scatter(grad_bv, ("gx", "gy"), scatter_dimension=0, tiled=True),
        lax.psum_scatter(grad_wo, ("gx", "gy"), scatter_dimension=0, tiled=True),
        lax.psum_scatter(grad_bo, ("gx", "gy"), scatter_dimension=0, tiled=True),
        lax.psum_scatter(grad_g2, ("gx", "gy"), scatter_dimension=0, tiled=True),
        lax.psum_scatter(grad_b2, ("gx", "gy"), scatter_dimension=0, tiled=True),
        lax.psum_scatter(grad_wup, ("gx", "gy"), scatter_dimension=0, tiled=True),
        lax.psum_scatter(grad_bup, ("gx", "gy"), scatter_dimension=0, tiled=True),
        lax.psum_scatter(grad_wdown, ("gx", "gy"), scatter_dimension=0, tiled=True),
        lax.psum_scatter(grad_bdown, ("gx", "gy"), scatter_dimension=0, tiled=True),
    )


def shards(
    tokens,
    lengths,
    key_mask,
    ln1_gain,
    ln1_bias,
    q_weight,
    q_bias,
    k_weight,
    v_weight,
    v_bias,
    o_weight,
    o_bias,
    ln2_gain,
    ln2_bias,
    up_weight,
    up_bias,
    down_weight,
    down_bias,
    out_grad,
):
    gathered = collect(
        ln1_gain,
        ln1_bias,
        q_weight,
        q_bias,
        k_weight,
        v_weight,
        v_bias,
        o_weight,
        o_bias,
        ln2_gain,
        ln2_bias,
        up_weight,
        up_bias,
        down_weight,
        down_bias,
    )
    row_count = tokens.shape[0]
    feature_count = tokens.shape[1]
    strip_count = lengths.shape[0]
    slot_count = row_count // strip_count
    head_count = feature_count // HEAD_DIM
    score_scale = 1.0 / math.sqrt(HEAD_DIM)
    slot_ids = lax.iota(jnp.int32, slot_count)
    visible = (slot_ids[None, :] == 0) | (slot_ids[None, :] < lengths[:, None]) & (key_mask == 1)

    def split_heads(values):
        return values.reshape(strip_count, slot_count, head_count, HEAD_DIM)

    gain_one = gathered[0].astype(jnp.float32)
    bias_one = gathered[1].astype(jnp.float32)
    gain_two = gathered[9].astype(jnp.float32)
    bias_two = gathered[10].astype(jnp.float32)
    inputs = tokens.astype(jnp.float32)
    normed = layer_norm(inputs, gain_one, bias_one).astype(jnp.bfloat16)
    queries = (right_mul(normed, gathered[2]) + gathered[3].astype(jnp.float32)).astype(
        jnp.bfloat16
    )
    key_rows = right_mul(normed, gathered[4]).astype(jnp.bfloat16)
    value_rows = (right_mul(normed, gathered[5]) + gathered[6].astype(jnp.float32)).astype(
        jnp.bfloat16
    )

    def attend(pieces):
        queries_in, keys_in, values_in, visible_in = pieces
        scores = (
            jnp.einsum("qhd,khd->hqk", queries_in, keys_in, preferred_element_type=jnp.float32)
            * score_scale
        )
        scores = jnp.where(visible_in[None, None, :], scores, NEG_FILL)
        row_max = jnp.max(scores, axis=-1, keepdims=True)
        powers = jnp.exp(scores - row_max)
        row_sum = jnp.sum(powers, axis=-1, keepdims=True)
        attn_low = (powers / row_sum).astype(jnp.bfloat16)
        context = jnp.einsum(
            "hqk,khd->qhd", attn_low, values_in, preferred_element_type=jnp.float32
        )
        return (context, row_max + jnp.log(row_sum))

    context, log_sums = lax.map(
        attend, (split_heads(queries), split_heads(key_rows), split_heads(value_rows), visible)
    )
    context = context.reshape(row_count, feature_count).astype(jnp.bfloat16)
    residual = inputs + right_mul(context, gathered[7]) + gathered[8].astype(jnp.float32)
    normed2 = layer_norm(residual, gain_two, bias_two).astype(jnp.bfloat16)
    hidden = right_mul(normed2, gathered[11]) + gathered[12].astype(jnp.float32)
    active = gelu_exact(hidden).astype(jnp.bfloat16)
    mlp_out = right_mul(active, gathered[13]) + gathered[14].astype(jnp.float32)
    block_out = (residual + mlp_out).astype(jnp.bfloat16)
    regathered = collect(
        ln1_gain,
        ln1_bias,
        q_weight,
        q_bias,
        k_weight,
        v_weight,
        v_bias,
        o_weight,
        o_bias,
        ln2_gain,
        ln2_bias,
        up_weight,
        up_bias,
        down_weight,
        down_bias,
    )
    cotangent = out_grad.astype(jnp.float32)
    grad_wdown = left_mul(active, out_grad)
    grad_bdown = jnp.sum(cotangent, axis=0)
    grad_active = back_mul(out_grad, regathered[13])
    _, gelu_pull = jax.vjp(gelu_exact, hidden)
    grad_hidden = gelu_pull(grad_active)[0].astype(jnp.bfloat16)
    grad_wup = left_mul(normed2, grad_hidden)
    grad_bup = jnp.sum(grad_hidden.astype(jnp.float32), axis=0)
    grad_normed2 = back_mul(grad_hidden, regathered[11])
    _, second_pull = jax.vjp(layer_norm, residual, gain_two, bias_two)
    grad_res, grad_g2, grad_b2 = second_pull(grad_normed2)
    grad_res = cotangent + grad_res
    grad_att = grad_res.astype(jnp.bfloat16)
    grad_wo = left_mul(context, grad_att)
    grad_bo = jnp.sum(grad_att.astype(jnp.float32), axis=0)
    grad_context = back_mul(grad_att, regathered[7]).astype(jnp.bfloat16)

    def attend_back(pieces):
        queries_in, keys_in, values_in, visible_in, lse_in, grad_in = pieces
        scores = (
            jnp.einsum("qhd,khd->hqk", queries_in, keys_in, preferred_element_type=jnp.float32)
            * score_scale
        )
        scores = jnp.where(visible_in[None, None, :], scores, NEG_FILL)
        attn_probs = jnp.exp(scores - lse_in)
        attn_low = attn_probs.astype(jnp.bfloat16)
        grad_values = jnp.einsum(
            "hqk,qhd->khd", attn_low, grad_in, preferred_element_type=jnp.float32
        )
        grad_probs = jnp.einsum(
            "qhd,khd->hqk", grad_in, values_in, preferred_element_type=jnp.float32
        )
        row_inner = jnp.sum(attn_probs * grad_probs, axis=-1, keepdims=True)
        grad_scores = (attn_probs * (grad_probs - row_inner)).astype(jnp.bfloat16)
        grad_queries = (
            jnp.einsum("hqk,khd->qhd", grad_scores, keys_in, preferred_element_type=jnp.float32)
            * score_scale
        )
        grad_keys = (
            jnp.einsum("hqk,qhd->khd", grad_scores, queries_in, preferred_element_type=jnp.float32)
            * score_scale
        )
        return (
            grad_queries.astype(jnp.bfloat16),
            grad_keys.astype(jnp.bfloat16),
            grad_values.astype(jnp.bfloat16),
        )

    grad_queries, grad_keys, grad_values = lax.map(
        attend_back,
        (
            split_heads(queries),
            split_heads(key_rows),
            split_heads(value_rows),
            visible,
            log_sums,
            split_heads(grad_context),
        ),
    )
    grad_queries = grad_queries.reshape(row_count, feature_count)
    grad_keys = grad_keys.reshape(row_count, feature_count)
    grad_values = grad_values.reshape(row_count, feature_count)
    grad_wq = left_mul(normed, grad_queries)
    grad_wk = left_mul(normed, grad_keys)
    grad_wv = left_mul(normed, grad_values)
    grad_bq = jnp.sum(grad_queries.astype(jnp.float32), axis=0)
    grad_bv = jnp.sum(grad_values.astype(jnp.float32), axis=0)
    grad_normed = (
        back_mul(grad_queries, regathered[2])
        + back_mul(grad_keys, regathered[4])
        + back_mul(grad_values, regathered[5])
    )
    _, first_pull = jax.vjp(layer_norm, inputs, gain_one, bias_one)
    grad_inputs, grad_g1, grad_b1 = first_pull(grad_normed)
    grad_tokens = grad_res + grad_inputs
    shares = spread_grads(
        grad_g1,
        grad_b1,
        grad_wq,
        grad_bq,
        grad_wk,
        grad_wv,
        grad_bv,
        grad_wo,
        grad_bo,
        grad_g2,
        grad_b2,
        grad_wup,
        grad_bup,
        grad_wdown,
        grad_bdown,
    )
    return (block_out, grad_tokens) + tuple(shares)


def solution(mesh):
    return jax.shard_map(
        shards,
        mesh=mesh,
        in_specs=(
            P(("gx", "gy"), None),
            P(("gx", "gy")),
            P(("gx", "gy"), None),
            P(("gx", "gy")),
            P(("gx", "gy")),
            P(("gx", "gy"), None),
            P(("gx", "gy")),
            P(("gx", "gy"), None),
            P(("gx", "gy"), None),
            P(("gx", "gy")),
            P(("gx", "gy"), None),
            P(("gx", "gy")),
            P(("gx", "gy")),
            P(("gx", "gy")),
            P(("gx", "gy"), None),
            P(("gx", "gy")),
            P(("gx", "gy"), None),
            P(("gx", "gy")),
            P(("gx", "gy"), None),
        ),
        out_specs=(
            P(("gx", "gy"), None),
            P(("gx", "gy"), None),
            P(("gx", "gy")),
            P(("gx", "gy")),
            P(("gx", "gy"), None),
            P(("gx", "gy")),
            P(("gx", "gy"), None),
            P(("gx", "gy"), None),
            P(("gx", "gy")),
            P(("gx", "gy"), None),
            P(("gx", "gy")),
            P(("gx", "gy")),
            P(("gx", "gy")),
            P(("gx", "gy"), None),
            P(("gx", "gy")),
            P(("gx", "gy"), None),
            P(("gx", "gy")),
        ),
        check_vma=False,
    )
```

profile of v0, /device:TPU:0, one launch (start us, length us, event | category | flops | bytes accessed | tf_op | source)
XLA Modules:
  0.0 1127.2 jit_solution(7891332789321585317)
XLA Ops:
  18.9 42.9 %all-reduce.19 = (bf16[768]{0:T(1024)(128)(2,1)S(1)}, bf16[768]{0:T(1024)(128)(2,1)S(1)}, bf16[768]{0:T(1024)(128)(2,1)S(1)}, bf16[768]{0:T(1024)(128)(2,1)S(1)}...) all-reduce(bf16[768]{0:T(1024)(128)(2,1)S(1)} %dynamic-update-slice, ...), channel_id=1, replica_groups=mesh['gx'=4,'gy'=8] {'gx','gy'}, use_global_device_ids=true, to_apply=%add.2 | all-reduce | flops 9216 | bytes 36864
  80.7 43.1 %all-gather.7.cloned.1.call-done = bf16[768,768]{1,0:T(8,128)(2,1)} async-done(((bf16[24,768]{1,0:T(8,128)(2,1)}), bf16[768,768]{1,0:T(8,128)(2,1)}) %all-gather.7.cloned.1.call-update) | async-done | bytes 1179664 | tf_op jit(solution)/shard_map/all_gather | solution.py:61
  140.8 38.7 %all-gather.9.cloned.1.call-done = bf16[768,768]{1,0:T(8,128)(2,1)} async-done(((bf16[24,768]{1,0:T(8,128)(2,1)}), bf16[768,768]{1,0:T(8,128)(2,1)}) %all-gather.9.cloned.1.call-update) | async-done | bytes 1179664 | tf_op jit(solution)/shard_map/all_gather | solution.py:58
  196.8 58.1 %while.26 = (s32[]{:T(128)}, bf16[2,529,12,64]{1,3,2,0:T(8,128)(2,1)}, f32[2,12,529,1]{2,1,3,0:T(8,128)S(1)}, bf16[2,529,12,64]{1,3,2,0:T(8,128)(2,1)}, pred[2,5...) while((s32[]{:T(128)}, ...), condition=%wide.region_5.6_spmd, body=%wide.region_2.5_spmd.sunk | while | flops 899962304 | bytes 54692004 | solution.py:190
  196.8 10.5 fusion.139
  207.4 9.3 fusion.140
  216.7 9.0 bitcast_dynamic-update-slice_fusion.4
  225.7 10.5 fusion.139
  236.3 9.3 fusion.140
  245.6 8.8 bitcast_dynamic-update-slice_fusion.4
  270.1 30.4 %all-gather.15.cloned.1.call-done = bf16[768,3072]{1,0:T(8,128)(2,1)} async-done(((bf16[24,3072]{1,0:T(8,128)(2,1)}), bf16[768,3072]{1,0:T(8,128)(2,1)}) %all-gather.15.cloned.1.call-update) | async-done | bytes 4718608 | tf_op jit(solution)/shard_map/all_gather | solution.py:67
  300.5 38.0 %multiply_convert_fusion.3 = (bf16[1058,3072]{1,0:T(8,128)(2,1)}, f32[1058,3072]{1,0:T(8,128)}, f32[1058,3072]{1,0:T(8,128)}) fusion(f32[3072]{0:T(1024)S(1)} %copy-done.40, bf16[768,3072]{1,0:T(8,128)(2,1)} %all-gather.15.cloned.1.call-done, f32[1058,768]{1,0:T(8,128)S(1)} %get-tuple-element.237, f32[768]{0:T(1024)S(1)} %copy-done.37, ...), kind=kOutput, calls=%fused_computation.61 | convolution fusion | flops 5210844672 | bytes 40497424 | tf_op jit(solution)/shard_map/dot_general | solution.py:23
  338.5 26.7 %all-gather.17.cloned.1.call-done = bf16[3072,768]{1,0:T(8,128)(2,1)} async-done(((bf16[96,768]{1,0:T(8,128)(2,1)}), bf16[3072,768]{1,0:T(8,128)(2,1)}) %all-gather.17.cloned.1.call-update) | async-done | bytes 4718608 | tf_op jit(solution)/shard_map/all_gather | solution.py:69
  365.2 19.3 %convert_reduce_fusion = (f32[3072]{0:T(1024)}, bf16[1058,3072]{1,0:T(8,128)(2,1)}) fusion(f32[1058,3072]{1,0:T(8,128)} %get-tuple-element.229, f32[1058,3072]{1,0:T(8,128)} %get-tuple-element.238, bf16[1058,768]{1,0:T(8,128)(2,1)} %param.41, bf16[3072,768]{1,0:T(8,128)(2,1)} %all-gather.17.cloned.1.call-done), kind=kOutput, calls=%fused_computation.59 | convolution fusion | flops 5044270080 | bytes 38857728 | tf_op jit(solution)/shard_map/dot_general | solution.py:33
  384.5 10.7 multiply_reduce_fusion.1
  416.3 100.3 %while.27 = (s32[]{:T(128)}, bf16[2,529,12,64]{1,3,2,0:T(8,128)(2,1)}, bf16[2,529,12,64]{1,3,2,0:T(8,128)(2,1)}, bf16[2,529,12,64]{1,3,2,0:T(8,128)(2,1)}, bf16[...) while((s32[]{:T(128)}, ...), condition=%wide.region_12.13_spmd, body=%wide.region_10.12_spmd.sunk | while | flops 2181426688 | bytes 142791664 | solution.py:265
  416.4 10.1 fusion.149
  426.5 12.3 %multiply_reduce_fusion.5 = (f32[12,529]{1,0:T(8,128)S(1)}, f32[12,529,529]{1,2,0:T(8,128)}) fusion(f32[12,529,529]{1,2,0:T(8,128)} %fusion.149, f32[12,529]{1,0:T(8,128)S(1)} %dynamic-slice_bitcast_fusion.2, bf16[2,529,12,64]{1,3,2,0:T(8,128)(2,1)S(1)} %get-tuple-element.407, s32[]{:T(128)S(6)} %copy.124, ...), kind=kOutput, calls=%fused_computation.21.clone.1 | convolution fusion | flops 446619840 | bytes 28899216 | tf_op jit(solution)/shard_map/while/body/eval_jaxpr/qhd,khd->hqk/dot_general | solution.py:237
  438.8 11.6 %multiply_convert_fusion.5 = bf16[12,529,529]{1,2,0:T(8,128)(2,1)S(1)} fusion(f32[12,529,529]{1,2,0:T(8,128)} %get-tuple-element.355, f32[12,529,529]{1,2,0:T(8,128)} %fusion.149, f32[12,529]{1,0:T(8,128)S(1)} %get-tuple-element.356), kind=kLoop, calls=%fused_computation.20.clone.1 | loop fusion | flops 10074276 | bytes 33606312 | tf_op jit(solution)/shard_map/while/body/eval_jaxpr/convert_element_type | solution.py:250
  450.5 9.4 fusion.152
  466.6 10.1 fusion.149
  476.7 12.3 %multiply_reduce_fusion.5 = (f32[12,529]{1,0:T(8,128)S(1)}, f32[12,529,529]{1,2,0:T(8,128)}) fusion(f32[12,529,529]{1,2,0:T(8,128)} %fusion.149, f32[12,529]{1,0:T(8,128)S(1)} %dynamic-slice_bitcast_fusion.2, bf16[2,529,12,64]{1,3,2,0:T(8,128)(2,1)S(1)} %get-tuple-element.407, s32[]{:T(128)S(6)} %copy.124, ...), kind=kOutput, calls=%fused_computation.21.clone.1 | convolution fusion | flops 446619840 | bytes 28899216 | tf_op jit(solution)/shard_map/while/body/eval_jaxpr/qhd,khd->hqk/dot_general | solution.py:237
  489.0 11.4 %multiply_convert_fusion.5 = bf16[12,529,529]{1,2,0:T(8,128)(2,1)S(1)} fusion(f32[12,529,529]{1,2,0:T(8,128)} %get-tuple-element.355, f32[12,529,529]{1,2,0:T(8,128)} %fusion.149, f32[12,529]{1,0:T(8,128)S(1)} %get-tuple-element.356), kind=kLoop, calls=%fused_computation.20.clone.1 | loop fusion | flops 10074276 | bytes 33606312 | tf_op jit(solution)/shard_map/while/body/eval_jaxpr/convert_element_type | solution.py:250
  500.4 9.3 fusion.152
  560.3 12.6 %fusion.75 = f32[768,3072]{1,0:T(8,128)} fusion(bf16[1058,3072]{1,0:T(8,128)(2,1)} %get-tuple-element.242, f32[1058,768]{1,0:T(8,128)} %copy-done.6, f32[768]{0:T(1024)S(1)} %copy-done.38, f32[768]{0:T(1024)S(1)} %copy-done.28, f32[1058]{0:T(1024)S(1)} %copy-done.26, f32[1058]{0:T(1024)S(1)} %copy-done.22), kind=kOutput, calls=%fused_computation.127 | convolution fusion | flops 4996333056 | bytes 19202320 | tf_op jit(solution)/shard_map/dot_general | solution.py:27
  573.2 11.2 fusion.92
  601.2 40.1 %all-reduce.18 = (f32[768]{0:T(1024)S(1)}, f32[768]{0:T(1024)S(1)}, f32[768]{0:T(1024)S(1)}, f32[768]{0:T(1024)S(1)}, f32[768]{0:T(1024)S(1)}, /*index=5*/f32[76...) all-reduce(f32[768]{0:T(1024)S(1)} %get-tuple-element.167, ...), channel_id=2, replica_groups=mesh['gx'=4,'gy'=8] {'gx','gy'}, use_global_device_ids=true, to_apply=%region_16.17.clone | all-reduce | flops 9216 | bytes 73728
  646.5 10.3 fusion.63
  656.8 75.6 %reduce-scatter.9.cloned.1.call-done = f32[24,768]{1,0:T(8,128)} async-done(((f32[768,768]{1,0:T(8,128)}), f32[24,768]{1,0:T(8,128)}) %reduce-scatter.9.cloned.1.call-update) | async-done | bytes 73744 | tf_op jit(solution)/shard_map/reduce_scatter | solution.py:96
  732.4 104.4 %reduce-scatter.7.cloned.1.call-done = f32[24,768]{1,0:T(8,128)} async-done(((f32[768,768]{1,0:T(8,128)}), f32[24,768]{1,0:T(8,128)}) %reduce-scatter.7.cloned.1.call-update) | async-done | bytes 73744 | tf_op jit(solution)/shard_map/reduce_scatter | solution.py:94
  836.8 141.6 %reduce-scatter.15.cloned.1.call-done = f32[24,3072]{1,0:T(8,128)} async-done(((f32[768,3072]{1,0:T(8,128)}), f32[24,3072]{1,0:T(8,128)}) %reduce-scatter.15.cloned.1.call-update) | async-done | bytes 294928 | tf_op jit(solution)/shard_map/reduce_scatter | solution.py:103
  978.4 141.4 %reduce-scatter.17.cloned.1.call-done = f32[96,768]{1,0:T(8,128)} async-done(((f32[3072,768]{1,0:T(8,128)}), f32[96,768]{1,0:T(8,128)}) %reduce-scatter.17.cloned.1.call-update) | async-done | bytes 294928 | tf_op jit(solution)/shard_map/reduce_scatter | solution.py:105
  (241 shorter events, 180.0 us)
Async XLA Ops:
  7.2 58.1 %copy-start.4 = (bf16[1058,768]{1,0:T(8,128)(2,1)S(1)}, bf16[1058,768]{1,0:T(8,128)(2,1)}, u32[]{:S(2)}) copy-start(bf16[1058,768]{1,0:T(8,128)(2,1)} %param.23) | copy-start | bytes 4875268
  7.2 59.4 %copy-start.42 = (s32[2,529]{1,0:T(2,128)S(1)}, s32[2,529]{1,0:T(2,128)}, u32[]{:S(2)}) copy-start(s32[2,529]{1,0:T(2,128)} %param.25) | copy-start | bytes 12700
  7.2 59.4 %copy-start.49 = (s32[2]{0:T(128)S(1)}, s32[2]{0:T(128)}, u32[]{:S(2)}) copy-start(s32[2]{0:T(128)} %param.24) | copy-start | bytes 28
  7.2 60.6 %all-gather.11.cloned.1.call-start = ((), (), s32[]{:S(2)}) async-start(), calls=%async_computation.8 | async-start | bytes 1216512 | tf_op jit(solution)/shard_map/all_gather | solution.py:60
  8.0 115.9 %all-gather.7.cloned.1.call-start = ((), (), s32[]{:S(2)}) async-start(), calls=%async_computation.6 | async-start | bytes 1216512 | tf_op jit(solution)/shard_map/all_gather | solution.py:61
  8.7 170.9 %all-gather.9.cloned.1.call-start = ((), (), s32[]{:S(2)}) async-start(), calls=%async_computation.7 | async-start | bytes 1216512 | tf_op jit(solution)/shard_map/all_gather | solution.py:58
  9.4 256.0 %all-gather.13.cloned.1.call-start = ((), (), s32[]{:S(2)}) async-start(), calls=%async_computation.9 | async-start | bytes 1216512 | tf_op jit(solution)/shard_map/all_gather | solution.py:63
  10.0 290.5 %all-gather.15.cloned.1.call-start = ((), (), s32[]{:S(2)}) async-start(), calls=%async_computation.10 | async-start | bytes 4866048 | tf_op jit(solution)/shard_map/all_gather | solution.py:67
  10.6 354.6 %all-gather.17.cloned.1.call-start = ((), (), s32[]{:S(2)}) async-start(), calls=%async_computation.11 | async-start | bytes 4866048 | tf_op jit(solution)/shard_map/all_gather | solution.py:69
  11.2 645.6 %reduce-scatter.13.cloned.1.call-start = ((), (), s32[]{:S(2)}) async-start(), calls=%async_computation.15 | async-start | bytes 2433024 | tf_op jit(solution)/shard_map/reduce_scatter | solution.py:99
  61.7 117.8 %copy-start.35 = (f32[768]{0:T(1024)}, f32[768]{0:T(1024)S(1)}, u32[]{:S(2)}) copy-start(f32[768]{0:T(1024)S(1)} %convert_element_type.111) | copy-start | bytes 9220
  61.7 117.8 %copy-start.43 = (f32[768]{0:T(1024)}, f32[768]{0:T(1024)S(1)}, u32[]{:S(2)}) copy-start(f32[768]{0:T(1024)S(1)} %convert_element_type.112) | copy-start | bytes 9220
  65.3 114.3 %copy-start.23 = (f32[1058]{0:T(1024)}, f32[1058]{0:T(1024)S(1)}, u32[]{:S(2)}) copy-start(f32[1058]{0:T(1024)S(1)} %broadcast_multiply_fusion.1) | copy-start | bytes 12700
  65.9 113.7 %copy-start.29 = (f32[1058]{0:T(1024)}, f32[1058]{0:T(1024)S(1)}, u32[]{:S(2)}) copy-start(f32[1058]{0:T(1024)S(1)} %fusion.72) | copy-start | bytes 12700
  254.9 10.5 copy-start
  254.9 10.5 copy-start.17
  254.9 10.5 copy-start.19
  254.9 10.5 copy-start.45
  269.5 125.7 %copy-start.6 = (f32[1058,768]{1,0:T(8,128)}, f32[1058,768]{1,0:T(8,128)S(1)}, u32[]{:S(2)}) copy-start(f32[1058,768]{1,0:T(8,128)S(1)} %get-tuple-element.237) | copy-start | bytes 9750532
  269.5 31.0 %copy-start.27 = (f32[768]{0:T(1024)S(1)}, f32[768]{0:T(1024)}, u32[]{:S(2)}) copy-start(f32[768]{0:T(1024)} %convert_element_type.122) | copy-start | bytes 9220
  269.5 31.0 %copy-start.37 = (f32[768]{0:T(1024)S(1)}, f32[768]{0:T(1024)}, u32[]{:S(2)}) copy-start(f32[768]{0:T(1024)} %convert_element_type.123) | copy-start | bytes 9220
  269.5 31.0 %copy-start.40 = (f32[3072]{0:T(1024)S(1)}, f32[3072]{0:T(1024)}, u32[]{:S(2)}) copy-start(f32[3072]{0:T(1024)} %convert_element_type.125) | copy-start | bytes 36868
  269.6 125.7 %copy-start.21 = (f32[1058]{0:T(1024)}, f32[1058]{0:T(1024)S(1)}, u32[]{:S(2)}) copy-start(f32[1058]{0:T(1024)S(1)} %broadcast_multiply_fusion) | copy-start | bytes 12700
  270.1 125.1 %copy-start.25 = (f32[1058]{0:T(1024)}, f32[1058]{0:T(1024)S(1)}, u32[]{:S(2)}) copy-start(f32[1058]{0:T(1024)S(1)} %fusion.73) | copy-start | bytes 12700
  402.2 254.6 %reduce-scatter.11.cloned.1.call-start = ((), (), s32[]{:S(2)}) async-start(), calls=%async_computation.14 | async-start | bytes 2433024 | tf_op jit(solution)/shard_map/reduce_scatter | solution.py:97
  416.4 10.1 copy-start.2
  438.8 11.7 %copy-start.3 = (bf16[2,529,12,64]{1,3,2,0:T(8,128)(2,1)S(1)}, bf16[2,529,12,64]{1,3,2,0:T(8,128)(2,1)}, u32[]{:S(2)}) copy-start(bf16[2,529,12,64]{1,3,2,0:T(8,128)(2,1)} %get-tuple-element.411) | copy-start | bytes 4875268 | tf_op jit(solution)/shard_map/while
  489.0 11.4 %copy-start.3 = (bf16[2,529,12,64]{1,3,2,0:T(8,128)(2,1)S(1)}, bf16[2,529,12,64]{1,3,2,0:T(8,128)(2,1)}, u32[]{:S(2)}) copy-start(bf16[2,529,12,64]{1,3,2,0:T(8,128)(2,1)} %get-tuple-element.411) | copy-start | bytes 4875268 | tf_op jit(solution)/shard_map/while
  529.5 202.9 %reduce-scatter.9.cloned.1.call-start = ((), (), s32[]{:S(2)}) async-start(), calls=%async_computation.13 | async-start | bytes 2433024 | tf_op jit(solution)/shard_map/reduce_scatter | solution.py:96
  544.7 292.1 %reduce-scatter.7.cloned.1.call-start = ((), (), s32[]{:S(2)}) async-start(), calls=%async_computation.12 | async-start | bytes 2433024 | tf_op jit(solution)/shard_map/reduce_scatter | solution.py:94
  560.2 418.1 %reduce-scatter.15.cloned.1.call-start = ((), (), s32[]{:S(2)}) async-start(), calls=%async_computation.16 | async-start | bytes 9732096 | tf_op jit(solution)/shard_map/reduce_scatter | solution.py:103
  572.9 546.9 %reduce-scatter.17.cloned.1.call-start = ((), (), s32[]{:S(2)}) async-start(), calls=%async_computation.17 | async-start | bytes 9732096 | tf_op jit(solution)/shard_map/reduce_scatter | solution.py:105
  (36 other events, 163.6 us)
Sparse Core Ops, SparseCore 0:
  10.9 56.8 all-gather.10
  70.7 53.0 all-gather.6
  126.7 52.8 all-gather.8
  182.3 52.8 all-gather.12
  237.9 62.4 all-gather.14
  303.2 61.9 all-gather.16
  402.3 97.9 reduce-scatter.12
  529.6 98.0 reduce-scatter.10
  633.6 98.7 reduce-scatter.8
  738.1 98.6 reduce-scatter.6
  843.2 135.1 reduce-scatter.14
  984.7 135.0 reduce-scatter.16
where the time goes:
time: 1130 us
  waiting for transfers between devices  607 us (54%)
  matrix products  260 us (23%)
  local copies, waits for them, and re-layouts  103 us (9%)
  blocking collectives  82.9 us (7%)
  other arithmetic  56.9 us (5%)
  between operations  15.4 us (1%)
    reduce_scatter x1, waiting for transfers between devices, spread_grads(): lax.psum_scatter(grad_wup, ('gx', 'gy'), scatter_dimension=0, tiled=True)  142 us
    reduce_scatter x1, waiting for transfers between devices, spread_grads(): lax.psum_scatter(grad_wdown, ('gx', 'gy'), scatter_dimension=0, tiled=True)  141 us
    reduce_scatter x1, waiting for transfers between devices, spread_grads(): lax.psum_scatter(grad_wq, ('gx', 'gy'), scatter_dimension=0, tiled=True)  104 us
    unnamed x2, blocking collectives  82.9 us
    reduce_scatter x1, waiting for transfers between devices, spread_grads(): lax.psum_scatter(grad_wk, ('gx', 'gy'), scatter_dimension=0, tiled=True)  75.6 us
    dot_general x6, matrix products, right_mul(): return jnp.dot(left_arg, right_arg, preferred_element_type=jnp.float32)  64.8 us
    all_gather x1, waiting for transfers between devices, collect(): lax.all_gather(v_weight, ('gx', 'gy'), axis=0, tiled=True)  43.1 us
    dot_general x6, matrix products, left_mul(): lax.dot_general(left_arg, right_arg, (((0,), (0,)), ((), ())), preferred_...  41.3 us
  transfers between devices with their start and end apart: 12, of which 9 were waited for; matrix products, arithmetic and copies ran while one was open for 34% of the time, Pallas kernels for 0%

commit v1 on v0

--- a/solution.py
+++ b/solution.py
@@ -7,6 +7,18 @@
 HEAD_DIM = 64
 EPSILON = 1e-06
 NEG_FILL = -1e30
+
+
+def gather_by_bits(x, axis, dim):
+    ways, here, turn = (lax.axis_size(axis), lax.axis_index(axis), x.shape[dim])
+    line, have = (x, 1)
+    while have < ways:
+        line = jnp.concatenate(
+            [line, lax.ppermute(line, axis, [(d, (d - have) % ways) for d in range(ways)])],
+            axis=dim,
+        )
+        have = 2 * have
+    return jnp.roll(line, here * turn, axis=dim)
 
 
 def layer_norm(values, gain_vec, bias_vec):
@@ -58,7 +70,7 @@
         lax.all_gather(q_weight, ("gx", "gy"), axis=0, tiled=True),
         lax.all_gather(q_bias, ("gx", "gy"), axis=0, tiled=True),
         lax.all_gather(k_weight, ("gx", "gy"), axis=0, tiled=True),
-        lax.all_gather(v_weight, ("gx", "gy"), axis=0, tiled=True),
+        gather_by_bits(v_weight, ("gx", "gy"), 0),
         lax.all_gather(v_bias, ("gx", "gy"), axis=0, tiled=True),
         lax.all_gather(o_weight, ("gx", "gy"), axis=0, tiled=True),
         lax.all_gather(o_bias, ("gx", "gy"), axis=0, tiled=True),

time: 1130 us -> 1100 us (0.973)
  waiting for transfers between devices: 607 us -> 559 us
  starting transfers between devices: 1.34 us -> 13.2 us
    all_gather x1 -> x0, waiting for transfers between devices: 43.1 us -> none  [collect(): lax.all_gather(v_weight, ('gx', 'gy'), axis=0, tiled=True)]
    all_gather x1, waiting for transfers between devices: 38.7 us -> 0.02 us  [collect(): lax.all_gather(q_weight, ('gx', 'gy'), axis=0, tiled=True)]
    ppermute x0 -> x5, waiting for transfers between devices: none -> 37.3 us  [gather_by_bits(): lax.ppermute(line, axis, [(d, (d - have) % ways) for d in range(ways)])]
    ppermute x0 -> x5, starting transfers between devices: none -> 11.9 us  [gather_by_bits(): lax.ppermute(line, axis, [(d, (d - have) % ways) for d in range(ways)])]
  transfers between devices with their start and end apart: 12 -> 16, of which waited for: 9 -> 10; matrix products, arithmetic and copies ran while one was open for 34% -> 34% of each run, Pallas kernels for 0% -> 0%
where the time goes in v1:
time: 1100 us; the launch traced here: 1090 us
  waiting for transfers between devices  559 us (51%)
  matrix products  256 us (23%)
  local copies, waits for them, and re-layouts  99.8 us (9%)
  blocking collectives  83.4 us (8%)
  other arithmetic  59.6 us (5%)
  between operations  15.1 us (1%)
  starting transfers between devices  13.2 us (1%)
    reduce_scatter x1, waiting for transfers between devices, spread_grads(): lax.psum_scatter(grad_wup, ('gx', 'gy'), scatter_dimension=0, tiled=True)  142 us
    reduce_scatter x1, waiting for transfers between devices, spread_grads(): lax.psum_scatter(grad_wdown, ('gx', 'gy'), scatter_dimension=0, tiled=True)  142 us
    reduce_scatter x1, waiting for transfers between devices, spread_grads(): lax.psum_scatter(grad_wq, ('gx', 'gy'), scatter_dimension=0, tiled=True)  105 us
    unnamed x2, blocking collectives  83.4 us
    reduce_scatter x1, waiting for transfers between devices, spread_grads(): lax.psum_scatter(grad_wk, ('gx', 'gy'), scatter_dimension=0, tiled=True)  80.8 us
    dot_general x6, matrix products, right_mul(): return jnp.dot(left_arg, right_arg, preferred_element_type=jnp.float32)  62.2 us
    dot_general x6, matrix products, back_mul(): lax.dot_general(left_arg, right_arg, (((1,), (1,)), ((), ())), preferred_...  40.7 us
    dot_general x6, matrix products, left_mul(): lax.dot_general(left_arg, right_arg, (((0,), (0,)), ((), ())), preferred_...  40 us
  transfers between devices with their start and end apart: 16, of which 10 were waited for; matrix products, arithmetic and copies ran while one was open for 34% of the time, Pallas kernels for 0%

profile of v1, /device:TPU:0, one launch (start us, length us, event | category | flops | bytes accessed | tf_op | source)
XLA Modules:
  0.0 1086.9 jit_solution(730299916113973539)
XLA Ops:
  32.5 43.6 %all-reduce.19 = (bf16[768]{0:T(1024)(128)(2,1)S(1)}, bf16[768]{0:T(1024)(128)(2,1)S(1)}, bf16[768]{0:T(1024)(128)(2,1)S(1)}, bf16[768]{0:T(1024)(128)(2,1)S(1)}...) all-reduce(bf16[768]{0:T(1024)(128)(2,1)S(1)} %dynamic-update-slice, ...), channel_id=1, replica_groups=mesh['gx'=4,'gy'=8] {'gx','gy'}, use_global_device_ids=true, to_apply=%add.2 | all-reduce | flops 9216 | bytes 36864
  82.3 7.5 collective-permute-done.3
  92.4 26.2 %collective-permute-done.4 = bf16[384,768]{1,0:T(8,128)(2,1)S(1)} collective-permute-done((bf16[384,768]{1,0:T(8,128)(2,1)S(1)}, bf16[384,768]{1,0:T(8,128)(2,1)S(1)}, u32[]{:S(2)}, u32[]{:S(2)}) %collective-permute-start.4) | collective-permute-done | bytes 589856 | tf_op jit(solution)/shard_map/ppermute | solution.py:17
  163.1 58.0 %while.26 = (s32[]{:T(128)}, bf16[2,529,12,64]{1,3,2,0:T(8,128)(2,1)}, f32[2,12,529,1]{2,1,3,0:T(8,128)S(1)}, bf16[2,529,12,64]{1,3,2,0:T(8,128)(2,1)}, pred[2,5...) while((s32[]{:T(128)}, ...), condition=%wide.region_5.7_spmd, body=%wide.region_2.6_spmd.sunk | while | flops 899962304 | bytes 54692004 | solution.py:202
  163.5 10.5 fusion.140
  174.1 9.3 fusion.141
  183.4 8.8 bitcast_dynamic-update-slice_fusion.4
  192.3 10.6 fusion.140
  202.8 9.5 fusion.141
  212.3 8.8 bitcast_dynamic-update-slice_fusion.4
  236.5 23.3 %all-gather.12.cloned.1.call-done = bf16[768,3072]{1,0:T(8,128)(2,1)} async-done(((bf16[24,3072]{1,0:T(8,128)(2,1)}), bf16[768,3072]{1,0:T(8,128)(2,1)}) %all-gather.12.cloned.1.call-update) | async-done | bytes 4718608 | tf_op jit(solution)/shard_map/all_gather | solution.py:79
  259.9 38.1 %multiply_convert_fusion.3 = (bf16[1058,3072]{1,0:T(8,128)(2,1)}, f32[1058,3072]{1,0:T(8,128)}, f32[1058,3072]{1,0:T(8,128)}) fusion(f32[3072]{0:T(1024)S(1)} %copy-done.44, bf16[768,3072]{1,0:T(8,128)(2,1)} %all-gather.12.cloned.1.call-done, f32[1058,768]{1,0:T(8,128)S(1)} %get-tuple-element.248, f32[768]{0:T(1024)S(1)} %copy-done.39, ...), kind=kOutput, calls=%fused_computation.61 | convolution fusion | flops 5210844672 | bytes 40497424 | tf_op jit(solution)/shard_map/dot_general | solution.py:35
  298.0 26.6 %all-gather.14.cloned.1.call-done = bf16[3072,768]{1,0:T(8,128)(2,1)} async-done(((bf16[96,768]{1,0:T(8,128)(2,1)}), bf16[3072,768]{1,0:T(8,128)(2,1)}) %all-gather.14.cloned.1.call-update) | async-done | bytes 4718608 | tf_op jit(solution)/shard_map/all_gather | solution.py:81
  324.6 19.3 %convert_reduce_fusion = (f32[3072]{0:T(1024)}, bf16[1058,3072]{1,0:T(8,128)(2,1)}) fusion(f32[1058,3072]{1,0:T(8,128)} %get-tuple-element.230, f32[1058,3072]{1,0:T(8,128)} %get-tuple-element.249, bf16[1058,768]{1,0:T(8,128)(2,1)} %param.43, bf16[3072,768]{1,0:T(8,128)(2,1)} %all-gather.14.cloned.1.call-done), kind=kOutput, calls=%fused_computation.59 | convolution fusion | flops 5044270080 | bytes 38857728 | tf_op jit(solution)/shard_map/dot_general | solution.py:45
  343.8 10.7 multiply_reduce_fusion.1
  375.7 100.4 %while.27 = (s32[]{:T(128)}, bf16[2,529,12,64]{1,3,2,0:T(8,128)(2,1)}, bf16[2,529,12,64]{1,3,2,0:T(8,128)(2,1)}, bf16[2,529,12,64]{1,3,2,0:T(8,128)(2,1)}, bf16[...) while((s32[]{:T(128)}, ...), condition=%wide.region_12.14_spmd, body=%wide.region_10.13_spmd.sunk | while | flops 2181426688 | bytes 142791664 | solution.py:277
  375.8 10.1 fusion.150
  385.9 12.3 %multiply_reduce_fusion.5 = (f32[12,529]{1,0:T(8,128)S(1)}, f32[12,529,529]{1,2,0:T(8,128)}) fusion(f32[12,529,529]{1,2,0:T(8,128)} %fusion.150, f32[12,529]{1,0:T(8,128)S(1)} %dynamic-slice_bitcast_fusion.2, bf16[2,529,12,64]{1,3,2,0:T(8,128)(2,1)S(1)} %get-tuple-element.418, s32[]{:T(128)S(6)} %copy.133, ...), kind=kOutput, calls=%fused_computation.21.clone.1 | convolution fusion | flops 446619840 | bytes 28899216 | tf_op jit(solution)/shard_map/while/body/eval_jaxpr/qhd,khd->hqk/dot_general | solution.py:249
  398.2 11.6 %multiply_convert_fusion.5 = bf16[12,529,529]{1,2,0:T(8,128)(2,1)S(1)} fusion(f32[12,529,529]{1,2,0:T(8,128)} %get-tuple-element.366, f32[12,529,529]{1,2,0:T(8,128)} %fusion.150, f32[12,529]{1,0:T(8,128)S(1)} %get-tuple-element.367), kind=kLoop, calls=%fused_computation.20.clone.1 | loop fusion | flops 10074276 | bytes 33606312 | tf_op jit(solution)/shard_map/while/body/eval_jaxpr/convert_element_type | solution.py:262
  409.9 9.4 fusion.153
  426.1 10.1 fusion.150
  436.1 12.3 %multiply_reduce_fusion.5 = (f32[12,529]{1,0:T(8,128)S(1)}, f32[12,529,529]{1,2,0:T(8,128)}) fusion(f32[12,529,529]{1,2,0:T(8,128)} %fusion.150, f32[12,529]{1,0:T(8,128)S(1)} %dynamic-slice_bitcast_fusion.2, bf16[2,529,12,64]{1,3,2,0:T(8,128)(2,1)S(1)} %get-tuple-element.418, s32[]{:T(128)S(6)} %copy.133, ...), kind=kOutput, calls=%fused_computation.21.clone.1 | convolution fusion | flops 446619840 | bytes 28899216 | tf_op jit(solution)/shard_map/while/body/eval_jaxpr/qhd,khd->hqk/dot_general | solution.py:249
  448.4 11.4 %multiply_convert_fusion.5 = bf16[12,529,529]{1,2,0:T(8,128)(2,1)S(1)} fusion(f32[12,529,529]{1,2,0:T(8,128)} %get-tuple-element.366, f32[12,529,529]{1,2,0:T(8,128)} %fusion.150, f32[12,529]{1,0:T(8,128)S(1)} %get-tuple-element.367), kind=kLoop, calls=%fused_computation.20.clone.1 | loop fusion | flops 10074276 | bytes 33606312 | tf_op jit(solution)/shard_map/while/body/eval_jaxpr/convert_element_type | solution.py:262
  459.9 9.3 fusion.153
  514.5 12.1 %fusion.78 = f32[768,3072]{1,0:T(8,128)} fusion(bf16[1058,3072]{1,0:T(8,128)(2,1)} %get-tuple-element.253, f32[1058,768]{1,0:T(8,128)S(1)} %copy-done.5, f32[768]{0:T(1024)S(1)} %copy-done.40, f32[768]{0:T(1024)S(1)} %copy-done.32, f32[1058]{0:T(1024)S(1)} %copy-done.28, f32[1058]{0:T(1024)S(1)} %copy-done.26), kind=kOutput, calls=%fused_computation.144 | convolution fusion | flops 4996333056 | bytes 19202320 | tf_op jit(solution)/shard_map/dot_general | solution.py:39
  526.9 11.2 %fusion.95 = f32[3072,768]{1,0:T(8,128)} fusion(bf16[1058,3072]{1,0:T(8,128)(2,1)} %get-tuple-element.229, bf16[1058,768]{1,0:T(8,128)(2,1)} %param.43), kind=kOutput, calls=%fused_computation.153 | convolution fusion | flops 4992270336 | bytes 17562624 | tf_op jit(solution)/shard_map/dot_general | solution.py:39
  556.0 39.8 %all-reduce.18 = (f32[768]{0:T(1024)S(1)}, f32[768]{0:T(1024)S(1)}, f32[768]{0:T(1024)S(1)}, f32[768]{0:T(1024)S(1)}, f32[768]{0:T(1024)S(1)}, /*index=5*/f32[76...) all-reduce(f32[768]{0:T(1024)S(1)} %get-tuple-element.168, ...), channel_id=2, replica_groups=mesh['gx'=4,'gy'=8] {'gx','gy'}, use_global_device_ids=true, to_apply=%region_16.18.clone | all-reduce | flops 9216 | bytes 73728
  601.1 9.8 fusion.63
  610.9 80.8 %reduce-scatter.9.cloned.1.call-done = f32[24,768]{1,0:T(8,128)} async-done(((f32[768,768]{1,0:T(8,128)}), f32[24,768]{1,0:T(8,128)}) %reduce-scatter.9.cloned.1.call-update) | async-done | bytes 73744 | tf_op jit(solution)/shard_map/reduce_scatter | solution.py:108
  691.7 104.6 %reduce-scatter.7.cloned.1.call-done = f32[24,768]{1,0:T(8,128)} async-done(((f32[768,768]{1,0:T(8,128)}), f32[24,768]{1,0:T(8,128)}) %reduce-scatter.7.cloned.1.call-update) | async-done | bytes 73744 | tf_op jit(solution)/shard_map/reduce_scatter | solution.py:106
  796.4 141.8 %reduce-scatter.15.cloned.1.call-done = f32[24,3072]{1,0:T(8,128)} async-done(((f32[768,3072]{1,0:T(8,128)}), f32[24,3072]{1,0:T(8,128)}) %reduce-scatter.15.cloned.1.call-update) | async-done | bytes 294928 | tf_op jit(solution)/shard_map/reduce_scatter | solution.py:115
  938.2 141.7 %reduce-scatter.17.cloned.1.call-done = f32[96,768]{1,0:T(8,128)} async-done(((f32[3072,768]{1,0:T(8,128)}), f32[96,768]{1,0:T(8,128)}) %reduce-scatter.17.cloned.1.call-update) | async-done | bytes 294928 | tf_op jit(solution)/shard_map/reduce_scatter | solution.py:117
  (269 shorter events, 189.9 us)
Async XLA Ops:
  7.2 84.5 %copy-start.8 = (bf16[1058,768]{1,0:T(8,128)(2,1)S(1)}, bf16[1058,768]{1,0:T(8,128)(2,1)}, u32[]{:S(2)}) copy-start(bf16[1058,768]{1,0:T(8,128)(2,1)} %param.25) | copy-start | bytes 4875268
  7.2 84.4 %copy-start.46 = (s32[2,529]{1,0:T(2,128)S(1)}, s32[2,529]{1,0:T(2,128)}, u32[]{:S(2)}) copy-start(s32[2,529]{1,0:T(2,128)} %param.27) | copy-start | bytes 12700
  7.2 84.4 %copy-start.55 = (s32[2]{0:T(128)S(1)}, s32[2]{0:T(128)}, u32[]{:S(2)}) copy-start(s32[2]{0:T(128)} %param.26) | copy-start | bytes 28
  7.2 125.9 %all-gather.8.cloned.1.call-start = ((), (), s32[]{:S(2)}) async-start(), calls=%async_computation.7 | async-start | bytes 1216512 | tf_op jit(solution)/shard_map/all_gather | solution.py:72
  8.0 138.1 %all-gather.6.cloned.1.call-start = ((), (), s32[]{:S(2)}) async-start(), calls=%async_computation.6 | async-start | bytes 1216512 | tf_op jit(solution)/shard_map/all_gather | solution.py:70
  8.7 223.2 %all-gather.10.cloned.1.call-start = ((), (), s32[]{:S(2)}) async-start(), calls=%async_computation.8 | async-start | bytes 1216512 | tf_op jit(solution)/shard_map/all_gather | solution.py:75
  9.4 250.4 %all-gather.12.cloned.1.call-start = ((), (), s32[]{:S(2)}) async-start(), calls=%async_computation.9 | async-start | bytes 4866048 | tf_op jit(solution)/shard_map/all_gather | solution.py:79
  10.0 314.5 %all-gather.14.cloned.1.call-start = ((), (), s32[]{:S(2)}) async-start(), calls=%async_computation.10 | async-start | bytes 4866048 | tf_op jit(solution)/shard_map/all_gather | solution.py:81
  10.1 8.4 collective-permute-start
  16.5 594.4 %reduce-scatter.13.cloned.1.call-start = ((), (), s32[]{:S(2)}) async-start(), calls=%async_computation.14 | async-start | bytes 2433024 | tf_op jit(solution)/shard_map/reduce_scatter | solution.py:111
  19.2 4.4 collective-permute-start.1
  20.1 126.0 %copy-start.29 = (f32[1058]{0:T(1024)}, f32[1058]{0:T(1024)S(1)}, u32[]{:S(2)}) copy-start(f32[1058]{0:T(1024)S(1)} %broadcast_multiply_fusion.1) | copy-start | bytes 12700
  24.4 55.0 %collective-permute-start.2 = (bf16[96,768]{1,0:T(8,128)(2,1)S(1)}, bf16[96,768]{1,0:T(8,128)(2,1)S(1)}, u32[]{:S(2)}, u32[]{:S(2)}) collective-permute-start(bf16[96,768]{1,0:T(8,128)(2,1)S(1)} %pad_maximum_fusion.1), channel_id=1, source_target_pairs={{0,28},{1,29},{2,30},{3,31},{4,0},{5,1},{6,2},{7,3},{8,4},{9,5},{1... | collective-permute-start | bytes 442376 | tf_op jit(solution)/shard_map/ppermute | solution.py:17
  76.1 70.0 %copy-start.41 = (f32[768]{0:T(1024)}, f32[768]{0:T(1024)S(1)}, u32[]{:S(2)}) copy-start(f32[768]{0:T(1024)S(1)} %convert_element_type.111) | copy-start | bytes 9220
  76.2 70.0 %copy-start.47 = (f32[768]{0:T(1024)}, f32[768]{0:T(1024)S(1)}, u32[]{:S(2)}) copy-start(f32[768]{0:T(1024)S(1)} %convert_element_type.112) | copy-start | bytes 9220
  80.1 9.6 collective-permute-start.3
  89.8 28.8 %collective-permute-start.4 = (bf16[384,768]{1,0:T(8,128)(2,1)S(1)}, bf16[384,768]{1,0:T(8,128)(2,1)S(1)}, u32[]{:S(2)}, u32[]{:S(2)}) collective-permute-start(bf16[384,768]{1,0:T(8,128)(2,1)S(1)} %get-tuple-element.237), channel_id=1, source_target_pairs={{0,16},{1,17},{2,18},{3,19},{4,20},{5,21},{6,22},{7,23},{8,24},{9,... | collective-permute-start | bytes 1769480 | tf_op jit(solution)/shard_map/ppermute | solution.py:17
  92.4 26.3 %copy-start.37 = (f32[1058]{0:T(1024)}, f32[1058]{0:T(1024)S(1)}, u32[]{:S(2)}) copy-start(f32[1058]{0:T(1024)S(1)} %fusion.69) | copy-start | bytes 12700
  92.4 53.7 %copy-start.33 = (f32[1058]{0:T(1024)}, f32[1058]{0:T(1024)S(1)}, u32[]{:S(2)}) copy-start(f32[1058]{0:T(1024)S(1)} %fusion.73) | copy-start | bytes 12700
  235.9 118.6 %copy-start.4 = (f32[1058,768]{1,0:T(8,128)}, f32[1058,768]{1,0:T(8,128)S(1)}, u32[]{:S(2)}) copy-start(f32[1058,768]{1,0:T(8,128)S(1)} %get-tuple-element.248) | copy-start | bytes 9750532
  235.9 23.9 %copy-start.31 = (f32[768]{0:T(1024)S(1)}, f32[768]{0:T(1024)}, u32[]{:S(2)}) copy-start(f32[768]{0:T(1024)} %convert_element_type.122) | copy-start | bytes 9220
  235.9 23.9 %copy-start.39 = (f32[768]{0:T(1024)S(1)}, f32[768]{0:T(1024)}, u32[]{:S(2)}) copy-start(f32[768]{0:T(1024)} %convert_element_type.123) | copy-start | bytes 9220
  235.9 23.9 %copy-start.44 = (f32[3072]{0:T(1024)S(1)}, f32[3072]{0:T(1024)}, u32[]{:S(2)}) copy-start(f32[3072]{0:T(1024)} %convert_element_type.125) | copy-start | bytes 36868
  236.0 118.6 %copy-start.25 = (f32[1058]{0:T(1024)}, f32[1058]{0:T(1024)S(1)}, u32[]{:S(2)}) copy-start(f32[1058]{0:T(1024)S(1)} %broadcast_multiply_fusion) | copy-start | bytes 12700
  236.5 118.0 %copy-start.27 = (f32[1058]{0:T(1024)}, f32[1058]{0:T(1024)S(1)}, u32[]{:S(2)}) copy-start(f32[1058]{0:T(1024)S(1)} %fusion.74) | copy-start | bytes 12700
  361.5 249.4 %reduce-scatter.11.cloned.1.call-start = ((), (), s32[]{:S(2)}) async-start(), calls=%async_computation.13 | async-start | bytes 2433024 | tf_op jit(solution)/shard_map/reduce_scatter | solution.py:109
  398.2 11.7 %copy-start.3 = (bf16[2,529,12,64]{1,3,2,0:T(8,128)(2,1)S(1)}, bf16[2,529,12,64]{1,3,2,0:T(8,128)(2,1)}, u32[]{:S(2)}) copy-start(bf16[2,529,12,64]{1,3,2,0:T(8,128)(2,1)} %get-tuple-element.422) | copy-start | bytes 4875268 | tf_op jit(solution)/shard_map/while
  448.4 11.4 %copy-start.3 = (bf16[2,529,12,64]{1,3,2,0:T(8,128)(2,1)S(1)}, bf16[2,529,12,64]{1,3,2,0:T(8,128)(2,1)}, u32[]{:S(2)}) copy-start(bf16[2,529,12,64]{1,3,2,0:T(8,128)(2,1)} %get-tuple-element.422) | copy-start | bytes 4875268 | tf_op jit(solution)/shard_map/while
  489.1 202.7 %reduce-scatter.9.cloned.1.call-start = ((), (), s32[]{:S(2)}) async-start(), calls=%async_computation.12 | async-start | bytes 2433024 | tf_op jit(solution)/shard_map/reduce_scatter | solution.py:108
  501.9 294.4 %reduce-scatter.7.cloned.1.call-start = ((), (), s32[]{:S(2)}) async-start(), calls=%async_computation.11 | async-start | bytes 2433024 | tf_op jit(solution)/shard_map/reduce_scatter | solution.py:106
  514.4 423.8 %reduce-scatter.15.cloned.1.call-start = ((), (), s32[]{:S(2)}) async-start(), calls=%async_computation.15 | async-start | bytes 9732096 | tf_op jit(solution)/shard_map/reduce_scatter | solution.py:115
  526.6 553.3 %reduce-scatter.17.cloned.1.call-start = ((), (), s32[]{:S(2)}) async-start(), calls=%async_computation.16 | async-start | bytes 9732096 | tf_op jit(solution)/shard_map/reduce_scatter | solution.py:117
  (46 other events, 239.5 us)
Sparse Core Ops, SparseCore 0:
  10.9 56.8 all-gather.7
  70.8 68.0 all-gather.5
  141.7 52.7 all-gather.9
  197.3 62.5 all-gather.11
  262.6 61.9 all-gather.13
  361.6 97.9 reduce-scatter.12
  489.2 97.9 reduce-scatter.10
  593.1 98.6 reduce-scatter.8
  697.6 98.6 reduce-scatter.6
  802.7 135.4 reduce-scatter.14
  944.7 135.1 reduce-scatter.16
